TPU v7x, 32 devices: a whole 2x2x4 slice. The times are simulated.
32 devices in a mesh: ctx: 8 (over y, x, core), wsh: 4 (over z).
Axes of the slice: x: 2, y: 2, z: 4, core: 2. Of those that a mesh axis runs over, the one named last changes fastest.
Arguments:
- tokens: bfloat16 [4, 1024, 1792], P('wsh', 'ctx'), may hold values from -6 to 6
- cotangent: bfloat16 [4, 1024, 1792], P('wsh', 'ctx'), may hold values from -6 to 6
- segment_ids: int32 [4, 1024], P('wsh'), may hold values from 0 to 23, never falling along the last dimension, each value on 1 to 256 neighbouring positions
- block_order: int32 [16], replicated, may hold values from 0 to 15, as said below
- premix: float32 [1792], P(('ctx', 'wsh')), may hold values from 0.5 to 1.5
- inward: float32 [1792, 2304], P(('ctx', 'wsh')), may hold values from -0.125 to 0.125
- filters: float32 [3, 1792], P(None, ('ctx', 'wsh')), may hold values from -4 to 4
- outward: float32 [1792, 1792], P(('ctx', 'wsh')), may hold values from -1 to 1
- prefeed: float32 [1792], P(('ctx', 'wsh')), may hold values from 0.5 to 1.5
- expand: float32 [1792, 9728], P(('ctx', 'wsh')), may hold values from -0.125 to 0.125
- shrink: float32 [4864, 1792], P(('ctx', 'wsh')), may hold values from -0.078125 to 0.078125
- premix_state: float32 [2, 1792], P(None, ('ctx', 'wsh')), may hold values from -30 to 100, as said below
- inward_state: float32 [2, 1792, 2304], P(None, ('ctx', 'wsh')), may hold values from -30 to 100, as said below
- filters_state: float32 [2, 3, 1792], P(None, None, ('ctx', 'wsh')), may hold values from -30 to 100, as said below
- outward_state: float32 [2, 1792, 1792], P(None, ('ctx', 'wsh')), may hold values from -30 to 100, as said below
- prefeed_state: float32 [2, 1792], P(None, ('ctx', 'wsh')), may hold values from -30 to 100, as said below
- expand_state: float32 [2, 1792, 9728], P(None, ('ctx', 'wsh')), may hold values from -30 to 100, as said below
- shrink_state: float32 [2, 4864, 1792], P(None, ('ctx', 'wsh')), may hold values from -30 to 100, as said below
Outputs:
- block_output: bfloat16 [4, 1024, 1792], P('wsh', 'ctx')
- input_grad: bfloat16 [4, 1024, 1792], P('wsh', 'ctx')
- premix_grad: float32 [1792], P(('ctx', 'wsh'))
- inward_grad: float32 [1792, 2304], P(('ctx', 'wsh'))
- filters_grad: float32 [3, 1792], P(None, ('ctx', 'wsh'))
- outward_grad: float32 [1792, 1792], P(('ctx', 'wsh'))
- prefeed_grad: float32 [1792], P(('ctx', 'wsh'))
- expand_grad: float32 [1792, 9728], P(('ctx', 'wsh'))
- shrink_grad: float32 [4864, 1792], P(('ctx', 'wsh'))
- premix_moments: float32 [2, 1792], P(None, ('ctx', 'wsh'))
- inward_moments: float32 [2, 1792, 2304], P(None, ('ctx', 'wsh'))
- filters_moments: float32 [2, 3, 1792], P(None, None, ('ctx', 'wsh'))
- outward_moments: float32 [2, 1792, 1792], P(None, ('ctx', 'wsh'))
- prefeed_moments: float32 [2, 1792], P(None, ('ctx', 'wsh'))
- expand_moments: float32 [2, 1792, 9728], P(None, ('ctx', 'wsh'))
- shrink_moments: float32 [2, 4864, 1792], P(None, ('ctx', 'wsh'))
- premix_master: float32 [1792], P(('ctx', 'wsh'))
- inward_master: float32 [1792, 2304], P(('ctx', 'wsh'))
- filters_master: float32 [3, 1792], P(None, ('ctx', 'wsh'))
- outward_master: float32 [1792, 1792], P(('ctx', 'wsh'))
- prefeed_master: float32 [1792], P(('ctx', 'wsh'))
- expand_master: float32 [1792, 9728], P(('ctx', 'wsh'))
- shrink_master: float32 [4864, 1792], P(('ctx', 'wsh'))
- weight_norms: float32 [2, 7], replicated
Inputs may be any that keep to these rules, and one draw needn't show every extreme that they name: `segment_ids`: each sequence's segment numbers never fall along positions and start at 0; a segment holds at most 256 positions and one holds exactly that many. `block_order`: A permutation of the 16 blocks; the two slots of each index of ctx hold blocks b and 15 - b for some b. `premix_state`: index 0 holds first moments, index 1 second moments, which are positive. `inward_state`: index 0 holds first moments, index 1 second moments, which are positive. `filters_state`: index 0 holds first moments, index 1 second moments, which are positive. `outward_state`: index 0 holds first moments, index 1 second moments, which are positive. `prefeed_state`: index 0 holds first moments, index 1 second moments, which are positive. `expand_state`: index 0 holds first moments, index 1 second moments, which are positive. `shrink_state`: index 0 holds first moments, index 1 second moments, which are positive.
All inputs are finite; a program needn't handle non-finite values.
Results may differ from a plain program's by a relative error of at most 0.013.
The roundings to bfloat16 on the way count: a program that leaves them out, or rounds other values in their place, can miss the bound.
Values may be sent and summed in bfloat16 or wider, within the bound.
A program may use at most 320 MiB of HBM per device.

v0:
```python
import jax
import jax.numpy as jnp
from jax import lax
from jax.sharding import PartitionSpec as P

HEADS = 16
QUERY_KEY_WIDTH = 16
KCONV = 3
STEP = 3
HDV = 112
QK = 256


norm_eps = 1e-05
adam_eps = 1e-08
beta_first = 0.9
beta_second = 0.99
learn_rate = 0.5


def inverse_rms(values):
    return lax.rsqrt(jnp.mean(values * values, axis=-1, keepdims=True) + norm_eps)


def rms_back(grad_normed, normed, scaler):
    return scaler * (grad_normed - normed * jnp.mean(grad_normed * normed, axis=-1, keepdims=True))


def silu_slope(values):
    sigmoid = jax.nn.sigmoid(values)
    return sigmoid * (1.0 + values * (1.0 - sigmoid))


def reorder(values, indices, blocks):
    columns = values.shape[-1]
    return jnp.take(values.reshape(blocks, -1, columns), indices, axis=0).reshape(-1, columns)


def body(
    tokens,
    cotangent,
    segment_ids,
    block_order,
    premix,
    inward,
    filters,
    outward,
    prefeed,
    expand,
    shrink,
    premix_state,
    inward_state,
    filters_state,
    outward_state,
    prefeed_state,
    expand_state,
    shrink_state,
):
    masters = (premix, inward, filters, outward, prefeed, expand, shrink)
    states = (
        premix_state,
        inward_state,
        filters_state,
        outward_state,
        prefeed_state,
        expand_state,
        shrink_state,
    )
    row_count = tokens.shape[1]
    model_width = tokens.shape[2]
    block_rows = row_count // 2
    blocks = block_order.shape[0]
    length = blocks * block_rows
    device = lax.axis_index("ctx")
    owned_blocks = lax.dynamic_slice_in_dim(block_order, 2 * device, 2, 0)
    local_pos = (
        owned_blocks[:, None] * block_rows + jnp.arange(block_rows, dtype=jnp.int32)[None, :]
    ).reshape(row_count)
    segments = segment_ids[0]
    local_seg = jnp.take(segments, local_pos)
    inverse = (
        jnp.zeros((blocks,), jnp.int32).at[block_order].set(jnp.arange(blocks, dtype=jnp.int32))
    )
    key_span = min(512, length)
    span_count = length // key_span
    score_scale = QUERY_KEY_WIDTH ** (-0.5)
    lowered = tuple((weight.astype(jnp.bfloat16) for weight in masters))
    gathered = (
        lax.all_gather(lowered[0], ("ctx", "wsh"), axis=0, tiled=True),
        lax.all_gather(lowered[1], ("ctx", "wsh"), axis=0, tiled=True),
        lax.all_gather(lowered[2], ("ctx", "wsh"), axis=1, tiled=True),
        lax.all_gather(lowered[3], ("ctx", "wsh"), axis=0, tiled=True),
        lax.all_gather(lowered[4], ("ctx", "wsh"), axis=0, tiled=True),
        lax.all_gather(lowered[5], ("ctx", "wsh"), axis=0, tiled=True),
        lax.all_gather(lowered[6], ("ctx", "wsh"), axis=0, tiled=True),
    )
    gain_one, inward_full, filter_full, outward_full, gain_two, expand_full, shrink_full = gathered
    inputs = tokens[0].astype(jnp.float32)
    scaler_one = inverse_rms(inputs)
    normed_one = inputs * scaler_one
    mixed_in = (normed_one * gain_one.astype(jnp.float32)).astype(jnp.bfloat16)
    project = jnp.dot(mixed_in, inward_full, preferred_element_type=jnp.float32)
    queries = project[:, :QK].astype(jnp.bfloat16)
    keys_own = project[:, QK : 2 * QK].astype(jnp.bfloat16)
    values_own = project[:, 2 * QK :].astype(jnp.bfloat16)
    keys_all, values_all = (
        lax.all_gather(keys_own, "ctx", axis=0, tiled=True),
        lax.all_gather(values_own, "ctx", axis=0, tiled=True),
    )
    keys_nat = reorder(keys_all, inverse, blocks)
    values_nat = reorder(values_all, inverse, blocks)
    taps_float = filter_full.astype(jnp.float32)
    sources = []
    usable = []
    tapped = []
    for offset in range(KCONV):
        source = jnp.maximum(local_pos - offset, 0)
        sources.append(source)
        usable.append(
            ((local_pos - offset >= 0) & (jnp.take(segments, source) == local_seg)).astype(
                jnp.float32
            )[:, None]
        )
        tapped.append(jnp.take(values_nat, source, axis=0).astype(jnp.float32) * usable[offset])
    convolved = jnp.zeros((row_count, model_width), jnp.float32)
    for offset in range(KCONV):
        convolved = convolved + taps_float[offset] * tapped[offset]
    query_head_rows = queries.reshape(row_count, HEADS, QUERY_KEY_WIDTH)

    def key_block(start_row, key_source, value_source):
        key_block_rows = lax.dynamic_slice_in_dim(key_source, start_row, key_span, 0).reshape(
            key_span, HEADS, QUERY_KEY_WIDTH
        )
        value_rows = lax.dynamic_slice_in_dim(value_source, start_row, key_span, 0).reshape(
            key_span, HEADS, HDV
        )
        key_pos = start_row + jnp.arange(key_span, dtype=jnp.int32)
        key_seg = lax.dynamic_slice_in_dim(segments, start_row, key_span, 0)
        allowed = (
            (key_pos[None, :] <= local_pos[:, None]) & (key_seg[None, :] == local_seg[:, None])
        ).astype(jnp.float32)
        attention_scores = (
            jnp.einsum(
                "rwb,nwb->wrn", query_head_rows, key_block_rows, preferred_element_type=jnp.float32
            )
            * score_scale
        )
        weights = (1.0 + attention_scores + 0.5 * attention_scores * attention_scores) * allowed[
            None
        ]
        return (key_block_rows, value_rows, allowed, attention_scores, weights)

    def forward_step(block_index, running):
        numerator, totals = running
        key_block_rows, value_rows, allowed, attention_scores, weights = key_block(
            block_index * key_span, keys_nat, values_nat
        )
        numerator = numerator + jnp.einsum(
            "hqk,khd->qhd",
            weights.astype(jnp.bfloat16),
            value_rows,
            preferred_element_type=jnp.float32,
        )
        return (numerator, totals + jnp.sum(weights, axis=2))

    numerator, totals = lax.fori_loop(
        0,
        span_count,
        forward_step,
        (
            jnp.zeros((row_count, HEADS, HDV), jnp.float32),
            jnp.zeros((HEADS, row_count), jnp.float32),
        ),
    )
    totals_rows = jnp.transpose(totals)[:, :, None]
    attended = numerator / totals_rows
    attended_flat = attended.reshape(row_count, model_width)
    conv_gate = jax.nn.silu(convolved)
    gated = (attended_flat * conv_gate).astype(jnp.bfloat16)
    residual = inputs + jnp.dot(gated, outward_full, preferred_element_type=jnp.float32)
    scaler_two = inverse_rms(residual)
    normed_two = residual * scaler_two
    feed_in = (normed_two * gain_two.astype(jnp.float32)).astype(jnp.bfloat16)
    gate_up = jnp.dot(feed_in, expand_full, preferred_element_type=jnp.float32)
    hidden_units = expand_full.shape[1] // 2
    gate_part = gate_up[:, :hidden_units]
    up_part = gate_up[:, hidden_units:]
    gate_silu = jax.nn.silu(gate_part)
    activated = (gate_silu * up_part).astype(jnp.bfloat16)
    block_output = (
        residual + jnp.dot(activated, shrink_full, preferred_element_type=jnp.float32)
    ).astype(jnp.bfloat16)
    regathered = (
        lax.all_gather(lowered[0], ("ctx", "wsh"), axis=0, tiled=True),
        lax.all_gather(lowered[1], ("ctx", "wsh"), axis=0, tiled=True),
        lax.all_gather(lowered[2], ("ctx", "wsh"), axis=1, tiled=True),
        lax.all_gather(lowered[3], ("ctx", "wsh"), axis=0, tiled=True),
        lax.all_gather(lowered[4], ("ctx", "wsh"), axis=0, tiled=True),
        lax.all_gather(lowered[5], ("ctx", "wsh"), axis=0, tiled=True),
        lax.all_gather(lowered[6], ("ctx", "wsh"), axis=0, tiled=True),
    )
    gain_one, inward_full, filter_full, outward_full, gain_two, expand_full, shrink_full = (
        regathered
    )
    keys_again, values_again = (
        lax.all_gather(keys_own, "ctx", axis=0, tiled=True),
        lax.all_gather(values_own, "ctx", axis=0, tiled=True),
    )
    keys_nat = reorder(keys_again, inverse, blocks)
    values_nat = reorder(values_again, inverse, blocks)
    taps_float = filter_full.astype(jnp.float32)
    grad_out = cotangent[0].astype(jnp.float32)
    grad_ffn = grad_out.astype(jnp.bfloat16)
    shrink_grad = jnp.einsum("tf,td->fd", activated, grad_ffn, preferred_element_type=jnp.float32)
    grad_act = jnp.einsum("td,fd->tf", grad_ffn, shrink_full, preferred_element_type=jnp.float32)
    grad_gate_up = jnp.concatenate(
        [grad_act * up_part * silu_slope(gate_part), grad_act * gate_silu], axis=1
    ).astype(jnp.bfloat16)
    expand_grad = jnp.einsum("td,tf->df", feed_in, grad_gate_up, preferred_element_type=jnp.float32)
    grad_feed = jnp.einsum(
        "tf,df->td", grad_gate_up, expand_full, preferred_element_type=jnp.float32
    )
    prefeed_grad = jnp.sum(grad_feed * normed_two, axis=0)
    grad_resid = grad_out + rms_back(
        grad_feed * gain_two.astype(jnp.float32), normed_two, scaler_two
    )
    grad_mix = grad_resid.astype(jnp.bfloat16)
    outward_grad = jnp.einsum("td,te->de", gated, grad_mix, preferred_element_type=jnp.float32)
    grad_gated = jnp.einsum("te,de->td", grad_mix, outward_full, preferred_element_type=jnp.float32)
    grad_attended = (grad_gated * conv_gate).reshape(row_count, HEADS, HDV)
    grad_conv = grad_gated * attended_flat * silu_slope(convolved)
    filters_grad = jnp.stack(
        [jnp.sum(grad_conv * tapped[offset], axis=0) for offset in range(KCONV)]
    )
    grad_numer = (grad_attended / totals_rows).astype(jnp.bfloat16)
    grad_totals = -jnp.transpose(jnp.sum(grad_attended * attended, axis=2)) / totals

    def query_step(block_index, grad_query):
        key_block_rows, value_rows, allowed, attention_scores, weights = key_block(
            block_index * key_span, keys_nat, values_nat
        )
        grad_weights = (
            jnp.einsum("qhd,khd->hqk", grad_numer, value_rows, preferred_element_type=jnp.float32)
            + grad_totals[:, :, None]
        )
        score_gradient = (grad_weights * (1.0 + attention_scores) * allowed[None]).astype(
            jnp.bfloat16
        )
        return (
            grad_query
            + jnp.einsum(
                "bzt,tbc->zbc", score_gradient, key_block_rows, preferred_element_type=jnp.float32
            )
            * score_scale
        )

    grad_query = lax.fori_loop(
        0, span_count, query_step, jnp.zeros((row_count, HEADS, QUERY_KEY_WIDTH), jnp.float32)
    )
    heads_own = grad_conv.reshape(2, block_rows, model_width)[:, : KCONV - 1].reshape(
        2 * (KCONV - 1), model_width
    )
    query_all, numer_all = (
        lax.all_gather(queries, "ctx", axis=0, tiled=True),
        lax.all_gather(grad_numer.reshape(row_count, model_width), "ctx", axis=0, tiled=True),
    )
    totals_all, heads_all = (
        lax.all_gather(jnp.transpose(grad_totals), "ctx", axis=0, tiled=True),
        lax.all_gather(heads_own, "ctx", axis=0, tiled=True),
    )
    heads_nat = reorder(heads_all, inverse, blocks).reshape(blocks, KCONV - 1, model_width)
    dealt_pos = (
        block_order[:, None] * block_rows + jnp.arange(block_rows, dtype=jnp.int32)[None, :]
    ).reshape(length)
    dealt_seg = jnp.take(segments, dealt_pos)
    key_heads = keys_own.reshape(row_count, HEADS, QUERY_KEY_WIDTH)
    value_heads = values_own.reshape(row_count, HEADS, HDV)

    def pull_step(block_index, running):
        grad_keys, grad_values = running
        start_row = block_index * key_span
        query_rows = lax.dynamic_slice_in_dim(query_all, start_row, key_span, 0).reshape(
            key_span, HEADS, QUERY_KEY_WIDTH
        )
        numer_rows = lax.dynamic_slice_in_dim(numer_all, start_row, key_span, 0).reshape(
            key_span, HEADS, HDV
        )
        total_rows = lax.dynamic_slice_in_dim(totals_all, start_row, key_span, 0)
        query_pos = lax.dynamic_slice_in_dim(dealt_pos, start_row, key_span, 0)
        query_seg = lax.dynamic_slice_in_dim(dealt_seg, start_row, key_span, 0)
        allowed = (
            (local_pos[None, :] <= query_pos[:, None]) & (local_seg[None, :] == query_seg[:, None])
        ).astype(jnp.float32)
        attention_scores = (
            jnp.einsum("rwb,nwb->wrn", query_rows, key_heads, preferred_element_type=jnp.float32)
            * score_scale
        )
        weights = (1.0 + attention_scores + 0.5 * attention_scores * attention_scores) * allowed[
            None
        ]
        grad_weights = (
            jnp.einsum("qhd,khd->hqk", numer_rows, value_heads, preferred_element_type=jnp.float32)
            + jnp.transpose(total_rows)[:, :, None]
        )
        score_gradient = (grad_weights * (1.0 + attention_scores) * allowed[None]).astype(
            jnp.bfloat16
        )
        grad_keys = (
            grad_keys
            + jnp.einsum(
                "ydp,dya->pya", score_gradient, query_rows, preferred_element_type=jnp.float32
            )
            * score_scale
        )
        grad_values = grad_values + jnp.einsum(
            "hqk,qhd->khd",
            weights.astype(jnp.bfloat16),
            numer_rows,
            preferred_element_type=jnp.float32,
        )
        return (grad_keys, grad_values)

    grad_keys, grad_values = lax.fori_loop(
        0,
        span_count,
        pull_step,
        (
            jnp.zeros((row_count, HEADS, QUERY_KEY_WIDTH), jnp.float32),
            jnp.zeros((row_count, HEADS, HDV), jnp.float32),
        ),
    )
    conv_blocks = grad_conv.reshape(2, block_rows, model_width)
    conv_parts = []
    for which in range(2):
        following = jnp.take(heads_nat, jnp.minimum(owned_blocks[which] + 1, blocks - 1), axis=0)
        extended = jnp.concatenate([conv_blocks[which], following], axis=0)
        block_pos = local_pos[which * block_rows : (which + 1) * block_rows]
        block_seg = local_seg[which * block_rows : (which + 1) * block_rows]
        added = jnp.zeros((block_rows, model_width), jnp.float32)
        for offset in range(KCONV):
            target = block_pos + offset
            valid = (
                (target < length)
                & (jnp.take(segments, jnp.minimum(target, length - 1)) == block_seg)
            ).astype(jnp.float32)[:, None]
            added = added + taps_float[offset] * extended[offset : offset + block_rows] * valid
        conv_parts.append(added)
    keys_grad_own = grad_keys.reshape(row_count, QK)
    values_grad_own = grad_values.reshape(row_count, model_width) + jnp.concatenate(
        conv_parts, axis=0
    )
    grad_project = jnp.concatenate(
        [grad_query.reshape(row_count, QK), keys_grad_own, values_grad_own], axis=1
    ).astype(jnp.bfloat16)
    inward_grad = jnp.einsum(
        "td,tp->dp", mixed_in, grad_project, preferred_element_type=jnp.float32
    )
    grad_mixin = jnp.einsum(
        "tp,dp->td", grad_project, inward_full, preferred_element_type=jnp.float32
    )
    premix_grad = jnp.sum(grad_mixin * normed_one, axis=0)
    input_grad = (
        grad_resid + rms_back(grad_mixin * gain_one.astype(jnp.float32), normed_one, scaler_one)
    ).astype(jnp.bfloat16)
    shards = (
        lax.psum_scatter(premix_grad, ("ctx", "wsh"), scatter_dimension=0, tiled=True),
        lax.psum_scatter(inward_grad, ("ctx", "wsh"), scatter_dimension=0, tiled=True),
        lax.psum_scatter(filters_grad, ("ctx", "wsh"), scatter_dimension=1, tiled=True),
        lax.psum_scatter(outward_grad, ("ctx", "wsh"), scatter_dimension=0, tiled=True),
        lax.psum_scatter(prefeed_grad, ("ctx", "wsh"), scatter_dimension=0, tiled=True),
        lax.psum_scatter(expand_grad, ("ctx", "wsh"), scatter_dimension=0, tiled=True),
        lax.psum_scatter(shrink_grad, ("ctx", "wsh"), scatter_dimension=0, tiled=True),
    )
    moments = []
    directions = []
    for state_pair, gradient in zip(states, shards):
        first_moment = beta_first * state_pair[0] + (1.0 - beta_first) * gradient
        second = beta_second * state_pair[1] + (1.0 - beta_second) * gradient * gradient
        directions.append(
            first_moment
            / (1.0 - beta_first**STEP)
            / (jnp.sqrt(second / (1.0 - beta_second**STEP)) + adam_eps)
        )
        moments.append(jnp.stack([first_moment, second]))
    step_sums = jnp.stack([jnp.sum(direction * direction) for direction in directions])
    weight_sums = jnp.stack([jnp.sum(weight * weight) for weight in masters])
    weight_total, step_total = lax.psum((weight_sums, step_sums), ("ctx", "wsh"))
    weight_norm = jnp.sqrt(weight_total)
    step_norm = jnp.sqrt(step_total)
    updated = [
        masters[position]
        - learn_rate * (weight_norm[position] / step_norm[position]) * directions[position]
        for position in range(7)
    ]
    weight_norms = jnp.stack([weight_norm, step_norm])
    return (
        block_output[None],
        input_grad[None],
        shards[0],
        shards[1],
        shards[2],
        shards[3],
        shards[4],
        shards[5],
        shards[6],
        moments[0],
        moments[1],
        moments[2],
        moments[3],
        moments[4],
        moments[5],
        moments[6],
        updated[0],
        updated[1],
        updated[2],
        updated[3],
        updated[4],
        updated[5],
        updated[6],
        weight_norms,
    )


def solution(mesh):
    placed = (
        P("wsh", "ctx", None),
        P("wsh", "ctx", None),
        P("wsh", None),
        P(),
        P(("ctx", "wsh")),
        P(("ctx", "wsh"), None),
        P(None, ("ctx", "wsh")),
        P(("ctx", "wsh"), None),
        P(("ctx", "wsh")),
        P(("ctx", "wsh"), None),
        P(("ctx", "wsh"), None),
        P(None, ("ctx", "wsh")),
        P(None, ("ctx", "wsh"), None),
        P(None, None, ("ctx", "wsh")),
        P(None, ("ctx", "wsh"), None),
        P(None, ("ctx", "wsh")),
        P(None, ("ctx", "wsh"), None),
        P(None, ("ctx", "wsh"), None),
    )
    return jax.shard_map(
        body,
        mesh=mesh,
        in_specs=placed,
        out_specs=(
            P("wsh", "ctx", None),
            P("wsh", "ctx", None),
            P(("ctx", "wsh")),
            P(("ctx", "wsh"), None),
            P(None, ("ctx", "wsh")),
            P(("ctx", "wsh"), None),
            P(("ctx", "wsh")),
            P(("ctx", "wsh"), None),
            P(("ctx", "wsh"), None),
            P(None, ("ctx", "wsh")),
            P(None, ("ctx", "wsh"), None),
            P(None, None, ("ctx", "wsh")),
            P(None, ("ctx", "wsh"), None),
            P(None, ("ctx", "wsh")),
            P(None, ("ctx", "wsh"), None),
            P(None, ("ctx", "wsh"), None),
            P(("ctx", "wsh")),
            P(("ctx", "wsh"), None),
            P(None, ("ctx", "wsh")),
            P(("ctx", "wsh"), None),
            P(("ctx", "wsh")),
            P(("ctx", "wsh"), None),
            P(("ctx", "wsh"), None),
            P(),
        ),
        check_vma=False,
    )
```

profile of v0, /device:TPU:0, one launch (start us, length us, event | category | flops | bytes accessed | tf_op | source)
XLA Modules:
  0.0 3371.8 jit_solution(18280142357958170861)
XLA Ops:
  7.2 2.6 multiply_reduce_fusion.12
  12.9 43.0 %all-reduce.8 = (bf16[1792]{0:T(1024)(128)(2,1)S(1)}, bf16[1792]{0:T(1024)(128)(2,1)S(1)}) all-reduce(bf16[1792]{0:T(1024)(128)(2,1)S(1)} %dynamic-update-slice.1, bf16[1792]{0:T(1024)(128)(2,1)S(1)} %dynamic-update-slice.2), channel_id=1, replica_groups=mesh['ctx'=8,'wsh'=4] {'ctx','wsh'}, use_global_device_ids=true, to_apply=%add | all-reduce | flops 3584 | bytes 14336
  57.1 33.7 all-gather.9.cloned.1.call-done
  90.8 4.8 convolution_convert_fusion
  97.3 2.5 multiply_reduce_fusion.14
  109.8 66.6 %all-gather = bf16[32,56,3]{1,2,0:T(4,128)(2,1)S(1)} all-gather(bf16[1,56,3]{1,2,0:T(4,128)(2,1)S(1)} %get-tuple-element.1197), channel_id=1, replica_groups=mesh['ctx'=8,'wsh'=4] {'ctx','wsh'}, dimensions={0}, use_global_device_ids=true | all-gather | bytes 11088 | tf_op jit(solution)/shard_map/all_gather | solution.py:91
  178.2 12.0 all_gather.51
  191.3 4.7 gather_fusion.2
  195.9 4.4 broadcast_select_fusion
  200.3 6.0 copy.106
  206.3 4.6 gather_fusion.9
  210.9 4.6 gather_fusion.7
  215.6 4.9 gather_fusion.5
  220.5 21.8 while.51
  223.2 3.3 fusion.183
  226.5 4.6 fusion.184
  233.8 3.3 fusion.183
  237.1 4.8 fusion.184
  245.2 2.9 multiply_convert_fusion.11
  248.1 4.4 multiply_reduce_fusion.10
  252.6 154.7 %all-gather.15.cloned.1.call-done = bf16[1792,9728]{1,0:T(8,128)(2,1)} async-done(((bf16[56,9728]{1,0:T(8,128)(2,1)}), bf16[1792,9728]{1,0:T(8,128)(2,1)}) %all-gather.15.cloned.1.call-update) | async-done | bytes 34865168 | tf_op jit(solution)/shard_map/all_gather | solution.py:94
  407.3 18.3 fusion.119
  425.6 100.4 %all-gather.17.cloned.1.call-done = bf16[4864,1792]{1,0:T(8,128)(2,1)} async-done(((bf16[152,1792]{1,0:T(8,128)(2,1)}), bf16[4864,1792]{1,0:T(8,128)(2,1)}) %all-gather.17.cloned.1.call-update) | async-done | bytes 17432592 | tf_op jit(solution)/shard_map/all_gather | solution.py:95
  526.0 11.5 multiply_convert_fusion.8
  537.5 18.5 multiply_reduce_fusion.4
  558.3 7.5 multiply_reduce_fusion.7
  566.0 6.6 fusion.85
  574.8 4.5 gather_fusion
  585.0 13.3 all_gather.57
  598.3 2.4 copy.110
  601.7 8.6 all-gather.1
  613.3 18.7 while.52
  615.0 2.8 fusion.190
  619.0 3.7 fusion.191
  624.4 2.8 fusion.190
  628.3 3.7 fusion.191
  632.2 9.0 all_gather.59
  644.0 35.7 %while.53 = (s32[]{:T(128)}, f32[128,16,16]{0,2,1:T(8,128)}, f32[128,16,112]{0,2,1:T(8,128)}, bf16[1024,256]{1,0:T(8,128)(2,1)}, bf16[1024,1792]{1,0:T(8,128)(2,...) while((s32[]{:T(128)}, f32[128,16,16]{0,2,1:T(8,128)}, ...), condition=%wide.region_11.16_spmd.clone, body=%wide.region_10.15_spmd.clone.sunk | while | flops 551321728 | bytes 50707240 | solution.py:323
  645.3 2.8 fusion.198
  648.2 2.3 copy.157
  651.8 5.6 fusion.199
  657.4 4.4 fusion.200
  662.9 2.8 fusion.198
  669.4 5.6 fusion.199
  675.0 4.7 fusion.200
  683.5 8.1 fusion.83
  693.0 13.8 fusion.76
  706.9 27.6 fusion.42
  734.5 4.6 stack.164
  739.3 9.3 fusion.40
  748.6 6.4 fusion.55
  755.0 42.3 %all-reduce.7 = (f32[1792]{0:T(1024)S(1)}, f32[3,1792]{1,0:T(4,128)S(1)}, f32[1792]{0:T(1024)S(1)}) all-reduce(f32[1792]{0:T(1024)S(1)} %get-tuple-element.1056, f32[3,1792]{1,0:T(4,128)S(1)} %pad_maximum_fusion.12, f32[1792]{0:T(1024)S(1)} %copy-done.36), channel_id=2, replica_groups=mesh['ctx'=8,'wsh'=4] {'ctx','wsh'}, use_global_device_ids=true, to_apply=%region_14.21.clone | all-reduce | flops 8960 | bytes 71680
  802.2 80.5 %reduce-scatter.11.cloned.1.call-done = f32[56,1792]{1,0:T(8,128)} async-done(((f32[1792,1792]{1,0:T(8,128)}), f32[56,1792]{1,0:T(8,128)}) %reduce-scatter.11.cloned.1.call-update) | async-done | bytes 401424 | tf_op jit(solution)/shard_map/reduce_scatter | solution.py:369
  882.7 2.9 multiply_reduce_fusion.13
  886.6 192.0 %reduce-scatter.9.cloned.1.call-done = f32[56,2304]{1,0:T(8,128)} async-done(((f32[1792,2304]{1,0:T(8,128)}), f32[56,2304]{1,0:T(8,128)}) %reduce-scatter.9.cloned.1.call-update) | async-done | bytes 516112 | tf_op jit(solution)/shard_map/reduce_scatter | solution.py:367
  1078.6 2.8 multiply_reduce_fusion.11
  1082.4 737.5 %reduce-scatter.13.cloned.1.call-done = f32[152,1792]{1,0:T(8,128)} async-done(((f32[4864,1792]{1,0:T(8,128)}), f32[152,1792]{1,0:T(8,128)}) %reduce-scatter.13.cloned.1.call-update) | async-done | bytes 1089552 | tf_op jit(solution)/shard_map/reduce_scatter | solution.py:372
  1819.9 4.0 multiply_reduce_fusion.2
  1823.9 1463.6 %reduce-scatter.15.cloned.1.call-done = f32[56,9728]{1,0:T(8,128)} async-done(((f32[1792,9728]{1,0:T(8,128)}), f32[56,9728]{1,0:T(8,128)}) %reduce-scatter.15.cloned.1.call-update) | async-done | bytes 2179088
  3287.5 7.1 multiply_reduce_fusion
  3294.7 4.7 stack.172
  3299.3 3.1 pad_maximum_fusion.2
  3302.4 39.7 %all-reduce.6 = (f32[7]{0:T(128)S(1)}, f32[7]{0:T(128)S(1)}) all-reduce(f32[7]{0:T(128)S(1)} %stack.164, f32[7]{0:T(128)S(1)} %stack.172), channel_id=1, replica_groups=mesh['ctx'=8,'wsh'=4] {'ctx','wsh'}, use_global_device_ids=true, to_apply=%region_32.39 | all-reduce | flops 14 | bytes 112 | tf_op jit(solution)/shard_map/psum | solution.py:387
  3353.0 4.8 pad_maximum_fusion
  (306 shorter events, 75.7 us)
Async XLA Ops:
  7.2 83.6 %all-gather.9.cloned.1.call-start = ((), (), s32[]{:S(2)}) async-start(), calls=%async_computation.4 | async-start | bytes 8515584 | tf_op jit(solution)/shard_map/all_gather | solution.py:90
  9.8 181.4 %all-gather.11.cloned.1.call-start = ((), (), s32[]{:S(2)}) async-start(), calls=%async_computation.5 | async-start | bytes 4128768 | tf_op jit(solution)/shard_map/all_gather | solution.py:108
  55.9 34.9 %copy-start.32 = (f32[1792]{0:T(1024)}, f32[1792]{0:T(1024)S(1)}, u32[]{:S(2)}) copy-start(f32[1792]{0:T(1024)S(1)} %convert_element_type.190) | copy-start | bytes 21508
  57.1 33.7 copy-start.37
  96.5 3.5 copy-start.6
  97.3 4.8 copy-start.10
  97.3 150.8 %all-gather.13.cloned.1.call-start = ((), (), s32[]{:S(2)}) async-start(), calls=%async_computation.6 | async-start | bytes 6623232 | tf_op jit(solution)/shard_map/all_gather | solution.py:92
  99.9 4.0 copy-start.50
  99.9 5.4 copy-start
  99.9 307.4 %all-gather.15.cloned.1.call-start = ((), (), s32[]{:S(2)}) async-start(), calls=%async_computation.7 | async-start | bytes 35954688 | tf_op jit(solution)/shard_map/all_gather | solution.py:94
  102.0 7.2 copy-start.39
  102.1 423.9 %all-gather.17.cloned.1.call-start = ((), (), s32[]{:S(2)}) async-start(), calls=%async_computation.8 | async-start | bytes 17977344 | tf_op jit(solution)/shard_map/all_gather | solution.py:95
  103.8 540.2 %all-gather.19.cloned.1.call-start = ((), (), s32[]{:S(2)}) async-start(), calls=%async_computation.9 | async-start | bytes 4128768 | tf_op jit(solution)/shard_map/all_gather | solution.py:265
  177.3 18.7 copy-start.45
  242.3 2.9 copy-start.34
  243.9 4.2 copy-start.14
  244.0 4.2 copy-start.3
  407.3 118.7 %copy-start.20 = (bf16[1,128,1792]{2,1,0:T(8,128)(2,1)S(1)}, bf16[1,128,1792]{2,1,0:T(8,128)(2,1)}, u32[]{:S(2)}) copy-start(bf16[1,128,1792]{2,1,0:T(8,128)(2,1)} %param.37) | copy-start | bytes 1376260
  556.1 1.8 copy-start.15
  556.1 1.8 copy-start.22
  556.1 1.8 copy-start.23
  556.1 2.0 copy-start.24
  556.1 2.3 copy-start.30
  557.8 8.1 copy-start.8
  565.9 316.8 %reduce-scatter.11.cloned.1.call-start = ((), (), s32[]{:S(2)}) async-start(), calls=%async_computation.11 | async-start | bytes 13246464 | tf_op jit(solution)/shard_map/reduce_scatter | solution.py:369
  572.6 506.0 %reduce-scatter.9.cloned.1.call-start = ((), (), s32[]{:S(2)}) async-start(), calls=%async_computation.10 | async-start | bytes 17031168 | tf_op jit(solution)/shard_map/reduce_scatter | solution.py:367
  579.4 4.6 copy-start.12
  583.8 28.1 copy-start.13
  598.3 15.0 copy-start.35
  613.3 27.9 copy-start.31
  613.3 27.9 copy-start.46
  645.3 2.8 copy-start.2
  651.8 5.6 copy-start.1
  662.9 2.8 copy-start.2
  669.4 5.6 copy-start.1
  679.7 3.8 copy-start.4
  679.7 3.8 copy-start.33
  679.7 3.8 copy-start.38
  683.5 8.1 copy-start.25
  691.7 1128.3 %reduce-scatter.13.cloned.1.call-start = ((), (), s32[]{:S(2)}) async-start(), calls=%async_computation.12 | async-start | bytes 35954688 | tf_op jit(solution)/shard_map/reduce_scatter | solution.py:372
  706.8 2580.7 %reduce-scatter.15.cloned.1.call-start = ((), (), s32[]{:S(2)}) async-start(), calls=%async_computation.13 | async-start | bytes 71909376
  734.5 4.7 copy-start.47
  734.5 4.7 copy-start.44
  734.5 4.7 copy-start.43
  734.5 4.7 copy-start.42
  739.3 9.3 copy-start.26
  748.6 6.4 copy-start.36
  748.6 50.0 %copy-start.48 = (f32[2,56]{1,0:T(2,128)S(1)}, f32[2,56]{1,0:T(2,128)}, u32[]{:S(2)}) copy-start(f32[2,56]{1,0:T(2,128)} %param.47) | copy-start | bytes 1348
  748.6 51.2 %copy-start.49 = (f32[2,56]{1,0:T(2,128)S(1)}, f32[2,56]{1,0:T(2,128)}, u32[]{:S(2)}) copy-start(f32[2,56]{1,0:T(2,128)} %param.51) | copy-start | bytes 1348
  748.6 52.5 %copy-start.9 = (f32[128,1792]{1,0:T(8,128)S(1)}, f32[128,1792]{1,0:T(8,128)}, u32[]{:S(2)}) copy-start(f32[128,1792]{1,0:T(8,128)} %copy-done.8) | copy-start | bytes 2752516
  798.0 87.6 %copy-start.41 = (f32[3,56]{1,0:T(4,128)}, f32[3,56]{1,0:T(4,128)S(1)}, u32[]{:S(2)}) copy-start(f32[3,56]{1,0:T(4,128)S(1)} %get-tuple-element.1145) | copy-start | bytes 2020
  799.3 86.4 %copy-start.53 = (f32[56]{0:T(128)}, f32[56]{0:T(128)S(1)}, u32[]{:S(2)}) copy-start(f32[56]{0:T(128)S(1)} %get-tuple-element.1151) | copy-start | bytes 676
  800.5 85.1 %copy-start.54 = (f32[56]{0:T(128)}, f32[56]{0:T(128)S(1)}, u32[]{:S(2)}) copy-start(f32[56]{0:T(128)S(1)} %get-tuple-element.1140) | copy-start | bytes 676
  802.2 276.3 %copy-start.29 = (f32[2,56,2304]{2,1,0:T(8,128)S(1)}, f32[2,56,2304]{2,1,0:T(8,128)}, u32[]{:S(2)}) copy-start(f32[2,56,2304]{2,1,0:T(8,128)} %param.48) | copy-start | bytes 3096580
  886.6 933.3 %copy-start.17 = (f32[2,152,1792]{2,1,0:T(8,128)S(1)}, f32[2,152,1792]{2,1,0:T(8,128)}, u32[]{:S(2)}) copy-start(f32[2,152,1792]{2,1,0:T(8,128)} %param.53) | copy-start | bytes 6537220
  3352.9 4.9 copy-start.51
  3353.0 5.4 copy-start.18
  3353.0 5.4 copy-start.19
  3353.0 6.2 copy-start.40
  3353.0 6.8 copy-start.27
  3353.0 6.8 copy-start.28
  3357.8 2.8 copy-start.52
  3357.8 3.3 copy-start.7
  3361.1 1.7 copy-start.11
  (3 other events, 3.5 us)
Sparse Core Ops, SparseCore 0:
  11.4 79.3 all-gather.8
  97.4 33.0 all-gather.10
  133.9 70.7 all-gather.12
  207.9 199.3 all-gather.14
  410.5 115.4 all-gather.16
  566.0 34.7 all-gather.18
  603.7 278.9 reduce-scatter.10
  889.7 188.8 reduce-scatter.8
  1081.4 738.4 reduce-scatter.12
  1822.7 1464.7 reduce-scatter.14
where the time goes:
time: 3380 us; the launch traced here: 3370 us
  waiting for transfers between devices  2760 us (82%)
  blocking collectives  234 us (7%)
  matrix products  192 us (6%)
  local copies, waits for them, and re-layouts  81.9 us (2%)
  other arithmetic  73.7 us (2%)
    unnamed x11, waiting for transfers between devices  1460 us
    reduce_scatter x1, waiting for transfers between devices, body(): lax.psum_scatter(shrink_grad, ('ctx', 'wsh'), scatter_dimension=0, tiled=...  738 us
    reduce_scatter x1, waiting for transfers between devices, body(): lax.psum_scatter(inward_grad, ('ctx', 'wsh'), scatter_dimension=0, tiled=...  192 us
    all_gather x1, waiting for transfers between devices, body(): lax.all_gather(lowered[5], ('ctx', 'wsh'), axis=0, tiled=True)  155 us
    all_gather x1, waiting for transfers between devices, body(): lax.all_gather(lowered[6], ('ctx', 'wsh'), axis=0, tiled=True)  100 us
    unnamed x2, blocking collectives  85.2 us
    reduce_scatter x1, waiting for transfers between devices, body(): lax.psum_scatter(outward_grad, ('ctx', 'wsh'), scatter_dimension=0, tiled...  80.5 us
  transfers between devices with their start and end apart: 10, of which 7 were waited for; matrix products, arithmetic and copies ran while one was open for 8% of the time, Pallas kernels for 0%

commit v1 on v0

v1 whole, which is shorter than its diff:
```python
import jax
import jax.numpy as jnp
from jax import lax
from jax.sharding import PartitionSpec as P

HEADS = 16
QUERY_KEY_WIDTH = 16
KCONV = 3
STEP = 3
HDV = 112
QK = 256
TILE = 128

norm_eps = 1e-05
adam_eps = 1e-08
beta_first = 0.9
beta_second = 0.99
learn_rate = 0.5

f32 = jnp.float32
bf16 = jnp.bfloat16
BOTH = ("ctx", "wsh")


def mm(left, right):
    return jnp.dot(left, right, preferred_element_type=f32)


def mm_nt(left, right):
    return lax.dot_general(left, right, (((1,), (1,)), ((), ())), preferred_element_type=f32)


def mm_tn(left, right):
    return lax.dot_general(left, right, (((0,), (0,)), ((), ())), preferred_element_type=f32)


def inverse_rms(values):
    return lax.rsqrt(jnp.mean(values * values, axis=-1, keepdims=True) + norm_eps)


def rms_back(grad_normed, normed, scaler):
    return scaler * (grad_normed - normed * jnp.mean(grad_normed * normed, axis=-1, keepdims=True))


def silu_slope(values):
    sigmoid = jax.nn.sigmoid(values)
    return sigmoid * (1.0 + values * (1.0 - sigmoid))


def gather_rows(values):
    return lax.all_gather(values, "ctx", axis=0, tiled=True)


def scatter_sum(values, ctx):
    rows, columns = values.shape
    pieces = lax.all_to_all(values.reshape(ctx, rows // ctx, columns), "ctx", 0, 0)
    return jnp.sum(pieces.astype(f32), axis=0)


def split_columns(shard, parts, ctx):
    rows = shard.shape[0]
    pieces, start = [], 0
    for width in parts:
        piece = shard[:, start : start + width].reshape(rows, ctx, width // ctx)
        pieces.append(piece)
        start += width
    return jnp.transpose(jnp.concatenate(pieces, axis=2), (1, 0, 2))


def join_columns(pieces, parts, ctx):
    moved = jnp.transpose(pieces, (1, 0, 2))
    rows, joined, start = moved.shape[0], [], 0
    for width in parts:
        own = width // ctx
        joined.append(moved[:, :, start : start + own].reshape(rows, width))
        start += own
    return jnp.concatenate(joined, axis=1)


def gather_columns(shard, parts, ctx):
    pieces = split_columns(shard, parts, ctx)
    rows, columns = pieces.shape[1:]
    swapped = lax.all_to_all(pieces, "ctx", 0, 0)
    full = lax.all_gather(swapped, "wsh", axis=1)
    return full.reshape(-1, columns)


def return_columns(grad, parts, ctx, wsh):
    columns = grad.shape[1]
    pieces = grad.astype(bf16).reshape(ctx, wsh, -1, columns)
    swapped = lax.all_to_all(pieces, "wsh", 1, 0)
    summed = jnp.sum(swapped.astype(f32), axis=0).astype(bf16)
    back = lax.all_to_all(summed, "ctx", 0, 0)
    return join_columns(back, parts, ctx).astype(f32)


def return_rows(grad, wsh):
    columns = grad.shape[1]
    pieces = grad.astype(bf16).reshape(wsh, -1, columns)
    swapped = lax.all_to_all(pieces, "wsh", 0, 0)
    return jnp.sum(swapped.astype(f32), axis=0)


def windows(values, prior):
    tiles = values.reshape((-1, TILE) + values.shape[1:])
    count = tiles.shape[0]
    padded = jnp.concatenate([jnp.zeros((prior,) + tiles.shape[1:], values.dtype), tiles], axis=0)
    return jnp.concatenate([padded[j : j + count] for j in range(prior + 1)], axis=1)


def unwindow(grads, prior):
    count = grads.shape[0]
    tail = grads.shape[2:]
    pieces = grads.reshape((count, prior + 1, TILE) + tail)
    total = jnp.zeros((count + prior, TILE) + tail, grads.dtype)
    for j in range(prior + 1):
        total = total.at[j : j + count].add(pieces[:, j])
    return total[prior:].reshape((count * TILE,) + tail)


def scores_of(query_tiles, key_windows, allowed):
    scores = jnp.einsum(
        "tqhd,tkhd->htqk", query_tiles, key_windows, preferred_element_type=f32
    ) * (QUERY_KEY_WIDTH ** (-0.5))
    return scores, (1.0 + scores + 0.5 * scores * scores) * allowed[None]


def allowed_of(segments, prior):
    length = segments.shape[0]
    positions = jnp.arange(length, dtype=jnp.int32)
    key_pos = jnp.arange(length, dtype=jnp.int32) + 1
    key_windows = windows(key_pos, prior)
    seg_windows = windows(segments, prior)
    pos_tiles = positions.reshape(-1, TILE)
    seg_tiles = segments.reshape(-1, TILE)
    return (
        (key_windows[:, None, :] >= 1)
        & (key_windows[:, None, :] - 1 <= pos_tiles[:, :, None])
        & (seg_windows[:, None, :] == seg_tiles[:, :, None])
    ).astype(f32)


def shifted(values, offset):
    if offset == 0:
        return values
    rows = values.shape[0]
    edge = jnp.zeros((abs(offset),) + values.shape[1:], values.dtype)
    if offset > 0:
        return jnp.concatenate([edge, values[: rows - offset]], axis=0)
    return jnp.concatenate([values[-offset:], edge], axis=0)


def make_body(ctx, wsh):
    def body(
        tokens, cotangent, segment_ids, block_order,
        premix, inward, filters, outward, prefeed, expand, shrink,
        premix_state, inward_state, filters_state, outward_state,
        prefeed_state, expand_state, shrink_state,
    ):
        masters = (premix, inward, filters, outward, prefeed, expand, shrink)
        states = (
            premix_state, inward_state, filters_state, outward_state,
            prefeed_state, expand_state, shrink_state,
        )
        width = tokens.shape[2]
        feed = expand.shape[1] // 2
        segments = segment_ids[0]
        length = segments.shape[0]
        blocks = block_order.shape[0]
        block_rows = length // blocks
        prior = -(-(length // 4 - 1) // TILE)
        heads = HEADS // ctx
        keys_width = QK // ctx
        own_values = width // ctx
        own_feed = feed // ctx
        inverse = (
            jnp.zeros((blocks,), jnp.int32).at[block_order].set(jnp.arange(blocks, dtype=jnp.int32))
        )

        def reorder(values, indices):
            return jnp.take(values.reshape(blocks, block_rows, -1), indices, axis=0).reshape(
                length, -1
            )

        in_parts, ex_parts = (QK, QK, width), (feed, feed)
        gains = lax.all_gather(
            jnp.stack([premix, prefeed]).astype(bf16), BOTH, axis=1, tiled=True
        ).astype(f32)
        gain_one, gain_two = gains[0], gains[1]
        taps = lax.all_gather(filters.astype(bf16), "wsh", axis=1, tiled=True).astype(f32)
        inward_own = gather_columns(inward.astype(bf16), in_parts, ctx)
        outward_own = lax.all_gather(outward.astype(bf16), "wsh", axis=0, tiled=True)
        expand_own = gather_columns(expand.astype(bf16), ex_parts, ctx)
        shrink_own = lax.all_gather(shrink.astype(bf16), "wsh", axis=0, tiled=True)
        tokens_all = gather_rows(tokens[0])
        grad_ffn = gather_rows(cotangent[0])

        inputs_all = tokens_all.astype(f32)
        mixed_in = (inputs_all * inverse_rms(inputs_all) * gain_one).astype(bf16)
        project = reorder(mm(mixed_in, inward_own).astype(bf16), inverse)
        queries = project[:, :keys_width].reshape(-1, TILE, heads, QUERY_KEY_WIDTH)
        keys = project[:, keys_width : 2 * keys_width].reshape(length, heads, QUERY_KEY_WIDTH)
        values = project[:, 2 * keys_width :]
        value_float = values.astype(f32)
        usable, tapped = [], []
        for offset in range(KCONV):
            usable.append(
                (
                    (shifted(segments, offset) == segments)
                    & (jnp.arange(length) >= offset)
                ).astype(f32)[:, None]
            )
            tapped.append(shifted(value_float, offset) * usable[offset])
        convolved = sum(taps[offset] * tapped[offset] for offset in range(KCONV))
        allowed = allowed_of(segments, prior)
        key_windows = windows(keys, prior)
        value_windows = windows(values.reshape(length, heads, HDV), prior)
        scores, weights = scores_of(queries, key_windows, allowed)
        probs = weights.astype(bf16)
        totals = jnp.sum(weights, axis=3)
        totals_rows = jnp.transpose(totals, (1, 2, 0))[..., None]
        numer = jnp.einsum("htqk,tkhd->tqhd", probs, value_windows, preferred_element_type=f32)
        attended = numer / totals_rows
        attended_flat = attended.reshape(length, own_values)
        conv_gate = jax.nn.silu(convolved)
        gated = reorder((attended_flat * conv_gate).astype(bf16), block_order)
        mixed_out = mm(gated, outward_own).astype(bf16)
        inputs = tokens[0].astype(f32)
        residual = inputs + scatter_sum(mixed_out, ctx)
        scaler_two = inverse_rms(residual)
        normed_two = residual * scaler_two
        feed_in = gather_rows((normed_two * gain_two).astype(bf16))

        gate_up = mm(feed_in, expand_own)
        gate_part, up_part = gate_up[:, :own_feed], gate_up[:, own_feed:]
        gate_silu = jax.nn.silu(gate_part)
        activated = (gate_silu * up_part).astype(bf16)
        block_output = (
            residual + scatter_sum(mm(activated, shrink_own).astype(bf16), ctx)
        ).astype(bf16)
        shrink_grad = mm_tn(activated, grad_ffn)
        grad_act = mm_nt(grad_ffn, shrink_own)
        grad_gate_up = jnp.concatenate(
            [grad_act * up_part * silu_slope(gate_part), grad_act * gate_silu], axis=1
        ).astype(bf16)
        expand_grad = mm_tn(feed_in, grad_gate_up)
        grad_feed = scatter_sum(mm_nt(grad_gate_up, expand_own).astype(bf16), ctx)
        prefeed_part = jnp.sum(grad_feed * normed_two, axis=0)
        grad_resid = cotangent[0].astype(f32) + rms_back(
            grad_feed * gain_two, normed_two, scaler_two
        )
        grad_mix = gather_rows(grad_resid.astype(bf16))

        outward_grad = mm_tn(gated, grad_mix)
        grad_gated = reorder(mm_nt(grad_mix, outward_own), inverse)
        grad_attended = (grad_gated * conv_gate).reshape(-1, TILE, heads, HDV)
        grad_conv = grad_gated * attended_flat * silu_slope(convolved)
        filters_part = jnp.stack(
            [jnp.sum(grad_conv * tapped[offset], axis=0) for offset in range(KCONV)]
        )
        grad_numer = (grad_attended / totals_rows).astype(bf16)
        grad_totals = -jnp.sum(grad_attended * attended, axis=3) / totals_rows[..., 0]
        grad_totals = jnp.transpose(grad_totals, (2, 0, 1))
        grad_weights = (
            jnp.einsum("tqhd,tkhd->htqk", grad_numer, value_windows, preferred_element_type=f32)
            + grad_totals[..., None]
        )
        score_gradient = (grad_weights * (1.0 + scores) * allowed[None]).astype(bf16)
        scale = QUERY_KEY_WIDTH ** (-0.5)
        grad_query = (
            jnp.einsum("htqk,tkhd->tqhd", score_gradient, key_windows, preferred_element_type=f32)
            * scale
        )
        grad_keys = (
            unwindow(
                jnp.einsum("htqk,tqhd->tkhd", score_gradient, queries, preferred_element_type=f32),
                prior,
            )
            * scale
        )
        grad_values = unwindow(
            jnp.einsum("htqk,tqhd->tkhd", probs, grad_numer, preferred_element_type=f32), prior
        ).reshape(length, own_values)
        for offset in range(KCONV):
            grad_values = grad_values + taps[offset] * shifted(
                grad_conv * usable[offset], -offset
            )
        grad_project = reorder(
            jnp.concatenate(
                [
                    grad_query.reshape(length, keys_width),
                    grad_keys.reshape(length, keys_width),
                    grad_values,
                ],
                axis=1,
            ).astype(bf16),
            block_order,
        )
        inward_grad = mm_tn(mixed_in, grad_project)
        grad_mixin = scatter_sum(mm_nt(grad_project, inward_own).astype(bf16), ctx)
        scaler_one = inverse_rms(inputs)
        normed_one = inputs * scaler_one
        premix_part = jnp.sum(grad_mixin * normed_one, axis=0)
        input_grad = (
            grad_resid + rms_back(grad_mixin * gain_one, normed_one, scaler_one)
        ).astype(bf16)

        gain_grads = lax.psum_scatter(
            jnp.stack([premix_part, prefeed_part]), BOTH, scatter_dimension=1, tiled=True
        )
        shards = (
            gain_grads[0],
            return_columns(inward_grad, in_parts, ctx, wsh),
            lax.psum_scatter(filters_part, "wsh", scatter_dimension=1, tiled=True),
            return_rows(outward_grad, wsh),
            gain_grads[1],
            return_columns(expand_grad, ex_parts, ctx, wsh),
            return_rows(shrink_grad, wsh),
        )
        return (block_output[None], input_grad[None]) + shards + update(masters, states, shards)

    return body


def update(masters, states, shards):
    moments = []
    directions = []
    for state_pair, gradient in zip(states, shards):
        first_moment = beta_first * state_pair[0] + (1.0 - beta_first) * gradient
        second = beta_second * state_pair[1] + (1.0 - beta_second) * gradient * gradient
        directions.append(
            first_moment
            / (1.0 - beta_first**STEP)
            / (jnp.sqrt(second / (1.0 - beta_second**STEP)) + adam_eps)
        )
        moments.append(jnp.stack([first_moment, second]))
    step_sums = jnp.stack([jnp.sum(direction * direction) for direction in directions])
    weight_sums = jnp.stack([jnp.sum(weight * weight) for weight in masters])
    totals = lax.psum(jnp.stack([weight_sums, step_sums]), BOTH)
    norms = jnp.sqrt(totals)
    updated = [
        masters[i] - learn_rate * (norms[0, i] / norms[1, i]) * directions[i] for i in range(7)
    ]
    return tuple(moments) + tuple(updated) + (norms,)


def solution(mesh):
    ctx, wsh = mesh.shape["ctx"], mesh.shape["wsh"]
    rows, columns, moments_rows = P(BOTH, None), P(None, BOTH), P(None, BOTH, None)
    vector, whole = P(BOTH), P("wsh", "ctx", None)
    weights = (vector, rows, columns, rows, vector, rows, rows)
    states = (
        columns, moments_rows, P(None, None, BOTH), moments_rows,
        columns, moments_rows, moments_rows,
    )
    return jax.shard_map(
        make_body(ctx, wsh),
        mesh=mesh,
        in_specs=(whole, whole, P("wsh", None), P()) + weights + states,
        out_specs=(whole, whole) + weights + states + weights + (P(),),
        check_vma=False,
    )
```

time: 3380 us -> 977 us (0.29)
  waiting for transfers between devices: 2760 us -> 358 us
  matrix products: 192 us -> 80.6 us
  starting transfers between devices: 0.41 us -> 52.7 us
    unnamed x11 -> x6, waiting for transfers between devices: 1460 us -> 0.76 us
    reduce_scatter x3 -> x0, waiting for transfers between devices: 1010 us -> none  [the longest x1 738 us: body(): lax.psum_scatter(shrink_grad, ('ctx', 'wsh'), scatter_dimension=0, tiled=...]
    all_to_all x0 -> x11, waiting for transfers between devices: none -> 239 us  [the longest x3 107 us: scatter_sum(): lax.all_to_all(values.reshape(ctx, rows // ctx, columns), 'ctx', 0, 0)]
    all_gather x6, waiting for transfers between devices: 289 us -> 119 us  [the longest x4 70.3 us: gather_rows(): return lax.all_gather(values, 'ctx', axis=0, tiled=True)]
    dot_general x26 -> x18, matrix products: 192 us -> 80.6 us  [the longest x4 26.3 us: mm_nt(): lax.dot_general(left, right, (((1,), (1,)), ((), ())), preferred_element_...]
    all_to_all x0 -> x11, starting transfers between devices: none -> 51.4 us  [the longest x3 13.8 us: scatter_sum(): lax.all_to_all(values.reshape(ctx, rows // ctx, columns), 'ctx', 0, 0)]
    all_to_all x0 -> x1, blocking collectives: none -> 47.2 us  [scatter_sum(): lax.all_to_all(values.reshape(ctx, rows // ctx, columns), 'ctx', 0, 0)]
    all_gather x5 -> x4, blocking collectives: 109 us -> 121 us  [the longest x1 69.3 us: body(): lax.all_gather(jnp.stack([premix, prefeed]).astype(bf16), BOTH, axis=1, t...]
  transfers between devices with their start and end apart: 10 -> 17, of which waited for: 7 -> 12; matrix products, arithmetic and copies ran while one was open for 8% -> 17% of each run, Pallas kernels for 0% -> 0%
where the time goes in v1:
time: 977 us; the launch traced here: 969 us
  waiting for transfers between devices  358 us (37%)
  blocking collectives  264 us (27%)
  local copies, waits for them, and re-layouts  96.8 us (10%)
  other arithmetic  90.9 us (9%)
  matrix products  80.6 us (8%)
  starting transfers between devices  52.7 us (5%)
  between operations  25.6 us (3%)
    all_to_all x3, waiting for transfers between devices, scatter_sum(): lax.all_to_all(values.reshape(ctx, rows // ctx, columns), 'ctx', 0, 0)  107 us
    all_to_all x2, waiting for transfers between devices, return_columns(): swapped = lax.all_to_all(pieces, 'wsh', 1, 0)  92.5 us
    all_gather x4, waiting for transfers between devices, gather_rows(): return lax.all_gather(values, 'ctx', axis=0, tiled=True)  70.3 us
    all_gather x1, blocking collectives, body(): lax.all_gather(jnp.stack([premix, prefeed]).astype(bf16), BOTH, axis=1, t...  69.3 us
    unnamed x2, blocking collectives  57.5 us
    all_to_all x1, blocking collectives, scatter_sum(): lax.all_to_all(values.reshape(ctx, rows // ctx, columns), 'ctx', 0, 0)  47.2 us
    psum x1, blocking collectives, update(): totals = lax.psum(jnp.stack([weight_sums, step_sums]), BOTH)  39.1 us
    all_gather x1, waiting for transfers between devices, body(): shrink_own = lax.all_gather(shrink.astype(bf16), 'wsh', axis=0, tiled=True)  38.6 us
  transfers between devices with their start and end apart: 17, of which 12 were waited for; matrix products, arithmetic and copies ran while one was open for 17% of the time, Pallas kernels for 0%

profile of v1, /device:TPU:0, one launch (start us, length us, event | category | flops | bytes accessed | tf_op | source)
XLA Modules:
  0.0 969.0 jit_solution(15023815569160416463)
XLA Ops:
  10.8 5.2 all-to-all-start
  16.7 69.3 %all-gather.4 = bf16[32,56,2]{1,2,0:T(2,128)(2,1)S(1)} all-gather(bf16[1,56,2]{1,2,0:T(2,128)(2,1)S(1)} %maximum_bitcast_fusion.2), channel_id=1, replica_groups=mesh['ctx'=8,'wsh'=4] {'ctx','wsh'}, dimensions={0}, use_global_device_ids=true | all-gather | bytes 7392 | tf_op jit(solution)/shard_map/all_gather | solution.py:186
  86.7 7.6 all-gather.5
  103.6 4.2 all-to-all-start.2
  109.2 18.9 %all_gather.41 = bf16[224,1792]{1,0:T(8,128)(2,1)} all-gather(bf16[56,1792]{1,0:T(8,128)(2,1)S(1)} %get-tuple-element.311), channel_id=1, replica_groups=mesh['ctx'=8,'wsh'=4] {'wsh'}, dimensions={0}, use_global_device_ids=true | all-gather | bytes 1003520 | tf_op jit(solution)/shard_map/all_gather | solution.py:192
  129.0 24.9 %all-gather.1 = bf16[8,224,288]{2,0,1:T(8,128)(2,1)S(1)} all-gather(bf16[8,56,288]{2,0,1:T(8,128)(2,1)S(1)} %copy.320), channel_id=3, replica_groups=mesh['ctx'=8,'wsh'=4] {'wsh'}, dimensions={1}, use_global_device_ids=true | all-gather | bytes 1290240 | tf_op jit(solution)/shard_map/all_gather | solution.py:84
  154.0 2.4 copy.321
  156.4 2.6 reshape.832
  159.4 3.0 fusion
  167.8 3.3 fusion.19
  184.7 47.2 %all_to_all.68 = bf16[8,128,1792]{2,1,0:T(8,128)(2,1)S(1)} all-to-all(bf16[8,128,1792]{2,1,0:T(8,128)(2,1)S(1)} %bitcast.354), channel_id=1, replica_groups=mesh['ctx'=8,'wsh'=4] {'ctx'}, dimensions={0} | all-to-all | bytes 7340032 | tf_op jit(solution)/shard_map/all_to_all | solution.py:56
  237.0 9.8 %all-gather.21.cloned.1.call-done = bf16[8,224,1216]{2,1,0:T(8,128)(2,1)} async-done(((bf16[8,56,1216]{2,1,0:T(8,128)(2,1)}), bf16[8,224,1216]{2,1,0:T(8,128)(2,1)}) %all-gather.21.cloned.1.call-update) | async-done | bytes 4358160 | tf_op jit(solution)/shard_map/all_gather | solution.py:84
  246.8 35.3 %all-gather.13.cloned.1.call-done = bf16[1024,1792]{1,0:T(8,128)(2,1)} async-done(((bf16[128,1792]{1,0:T(8,128)(2,1)}), bf16[1024,1792]{1,0:T(8,128)(2,1)}) %all-gather.13.cloned.1.call-update) | async-done | bytes 3670032 | tf_op jit(solution)/shard_map/all_gather | solution.py:51
  282.1 10.4 %fusion.142 = f32[1024,1216]{0,1:T(8,128)} fusion(bf16[1024,1792]{1,0:T(8,128)(2,1)} %all-gather.13.cloned.1.call-done, bf16[1792,1216]{1,0:T(8,128)(2,1)} %bitcast.412), kind=kOutput, calls=%fused_computation.307 | convolution fusion | flops 4462739456 | bytes 13008896 | tf_op jit(solution)/shard_map/dot_general | solution.py:26
  292.5 38.6 %all-gather.15.cloned.1.call-done = bf16[608,1792]{1,0:T(8,128)(2,1)} async-done(((bf16[152,1792]{1,0:T(8,128)(2,1)}), bf16[608,1792]{1,0:T(8,128)(2,1)}) %all-gather.15.cloned.1.call-update) | async-done | bytes 2179088 | tf_op jit(solution)/shard_map/all_gather | solution.py:194
  331.1 34.9 %all-gather.23.cloned.1.call-done = bf16[1,1024,1792]{2,1,0:T(8,128)(2,1)} async-done(((bf16[1,128,1792]{2,1,0:T(8,128)(2,1)}), bf16[1,1024,1792]{2,1,0:T(8,128)(2,1)}) %all-gather.23.cloned.1.call-update) | async-done | bytes 3670032 | tf_op jit(solution)/shard_map/all_gather | solution.py:51
  366.1 8.4 multiply_convert_fusion.2
  374.4 9.7 convolution_convert_fusion.2
  384.1 4.7 all-to-all-start.4
  388.8 6.9 convolution_convert_fusion.3
  395.8 36.6 %all-to-all-done.4 = bf16[8,128,1792]{2,1,0:T(8,128)(2,1)} async-done(((bf16[8,128,1792]{2,1,0:T(8,128)(2,1)}), bf16[8,128,1792]{2,1,0:T(8,128)(2,1)}, u32[]{:S(2)}, u32[]{:S(2)}) %all-to-all-start.4) | async-done | bytes 3670048 | tf_op jit(solution)/shard_map/all_to_all | solution.py:56
  432.3 4.5 all-to-all-start.3
  436.8 6.2 fusion.7
  443.0 37.3 %all-to-all-done.3 = bf16[8,128,1792]{2,1,0:T(8,128)(2,1)} async-done(((bf16[8,128,1792]{2,1,0:T(8,128)(2,1)}), bf16[8,128,1792]{2,1,0:T(8,128)(2,1)}, u32[]{:S(2)}, u32[]{:S(2)}) %all-to-all-start.3) | async-done | bytes 3670048 | tf_op jit(solution)/shard_map/all_to_all | solution.py:56
  480.3 4.6 all-to-all-start.11
  484.9 9.6 convolution_convert_fusion
  494.5 7.2 copy.370
  501.6 4.7 copy.371
  506.4 25.8 %all-to-all-done.11 = bf16[4,152,1792]{2,1,0:T(8,128)(2,1)} async-done(((bf16[4,152,1792]{2,1,0:T(8,128)(2,1)}), bf16[4,152,1792]{2,1,0:T(8,128)(2,1)}, u32[]{:S(2)}, u32[]{:S(2)}) %all-to-all-start.11) | async-done | bytes 2179104 | tf_op jit(solution)/shard_map/all_to_all | solution.py:100
  532.1 4.9 all-to-all-start.9
  537.3 2.6 convert_reduce_fusion.1
  545.4 5.0 stack.155
  552.1 3.8 convert_reduce_fusion.2
  557.9 80.3 %all-to-all-done.9 = bf16[1,8,4,56,1216]{4,3,1,0,2:T(8,128)(2,1)} async-done(((bf16[1,8,4,56,1216]{4,3,1,0,2:T(8,128)(2,1)}), bf16[1,8,4,56,1216]{4,3,1,0,2:T(8,128)(2,1)}, u32[]{:S(2)}, u32[]{:S(2)}) %all-to-all-start.9) | async-done | bytes 4358176 | tf_op jit(solution)/shard_map/all_to_all | solution.py:91
  638.2 4.4 reduce_sum.346
  642.6 4.9 all-to-all-start.10
  654.2 9.9 %all-to-all-done.10 = bf16[8,56,1216]{2,1,0:T(8,128)(2,1)} async-done(((bf16[8,56,1216]{2,1,0:T(8,128)(2,1)}), bf16[8,56,1216]{2,1,0:T(8,128)(2,1)}, u32[]{:S(2)}, u32[]{:S(2)}) %all-to-all-start.10) | async-done | bytes 1089568 | tf_op jit(solution)/shard_map/all_to_all | solution.py:93
  667.9 2.4 concatenate.156
  670.3 4.4 fusion.143
  674.6 2.9 gather_fusion.1
  677.6 4.4 multiply_reduce_fusion.6
  696.4 3.9 copy.354
  704.7 2.8 reshape.927
  722.0 4.5 convolution_convert_fusion.5
  729.5 4.3 all-to-all-start.6
  733.8 4.5 fusion.11
  738.4 2.4 reshape.859
  740.7 2.4 reshape.858
  743.1 6.9 multiply_reduce_fusion
  751.9 12.1 %all-to-all-done.6 = bf16[1,8,4,56,288]{4,3,1,0,2:T(8,128)(2,1)} async-done(((bf16[1,8,4,56,288]{4,3,1,0,2:T(8,128)(2,1)}), bf16[1,8,4,56,288]{4,3,1,0,2:T(8,128)(2,1)}, u32[]{:S(2)}, u32[]{:S(2)}) %all-to-all-start.6) | async-done | bytes 1032224 | tf_op jit(solution)/shard_map/all_to_all | solution.py:91
  764.0 4.2 all-to-all-start.8
  768.3 4.0 pad_maximum_fusion
  772.3 15.3 %all-reduce.12 = f32[3,224]{1,0:T(4,128)} all-reduce(f32[3,224]{1,0:T(4,128)S(1)} %pad_maximum_fusion.13), channel_id=7, replica_groups=mesh['ctx'=8,'wsh'=4] {'wsh'}, use_global_device_ids=true, to_apply=%region_19.21.clone | all-reduce | flops 672 | bytes 5376
  787.6 2.4 reduce_sum.341
  790.0 5.2 all-to-all-start.7
  795.2 3.9 convolution_convert_fusion.1
  799.2 3.8 all-to-all-done.7
  803.0 4.6 all-to-all-start.5
  818.2 32.9 %all-to-all-done.5 = bf16[8,128,1792]{2,1,0:T(8,128)(2,1)} async-done(((bf16[8,128,1792]{2,1,0:T(8,128)(2,1)}), bf16[8,128,1792]{2,1,0:T(8,128)(2,1)}, u32[]{:S(2)}, u32[]{:S(2)}) %all-to-all-start.5) | async-done | bytes 3670048 | tf_op jit(solution)/shard_map/all_to_all | solution.py:56
  851.1 2.6 convert_reduce_fusion
  854.1 42.1 %all-reduce.11 = f32[2,1792]{1,0:T(2,128)S(1)} all-reduce(f32[2,1792]{1,0:T(2,128)S(1)} %pad_maximum_fusion.12), channel_id=6, replica_groups=mesh['ctx'=8,'wsh'=4] {'ctx','wsh'}, use_global_device_ids=true, to_apply=%region_14.16.clone | all-reduce | flops 3584 | bytes 28672
  897.5 4.6 stack.164
  902.1 39.1 %psum.7 = f32[2,7]{1,0:T(2,128)S(1)} all-reduce(f32[2,7]{1,0:T(2,128)S(1)} %pad_maximum_fusion.17), channel_id=1, replica_groups=mesh['ctx'=8,'wsh'=4] {'ctx','wsh'}, use_global_device_ids=true, to_apply=%region_37.39 | all-reduce | flops 14 | bytes 112 | tf_op jit(solution)/shard_map/psum | solution.py:339
  951.0 3.0 fusion.70
  (389 shorter events, 118.4 us)
Async XLA Ops:
  7.2 152.1 %all-gather.19.cloned.1.call-start = ((), (), s32[]{:S(2)}) async-start(), calls=%async_computation.15 | async-start | bytes 4128768 | tf_op jit(solution)/shard_map/all_gather | solution.py:51
  7.9 8.1 copy-start.93
  7.9 8.1 copy-start.95
  9.3 76.8 %copy-start.70 = (f32[3,56]{1,0:T(4,128)S(1)}, f32[3,56]{1,0:T(4,128)}, u32[]{:S(2)}) copy-start(f32[3,56]{1,0:T(4,128)} %param.38) | copy-start | bytes 2020
  9.3 85.0 %copy-start.8 = (f32[56,9728]{1,0:T(8,128)S(1)}, f32[56,9728]{1,0:T(8,128)}, u32[]{:S(2)}) copy-start(f32[56,9728]{1,0:T(8,128)} %param.41) | copy-start | bytes 6537220
  10.8 92.8 %all-to-all-start = ((bf16[8,56,288]{2,1,0:T(8,128)(2,1)}), bf16[8,56,288]{2,1,0:T(8,128)(2,1)}, u32[]{:S(2)}, u32[]{:S(2)}) async-start(bf16[8,56,288]{2,1,0:T(8,128)(2,1)} %maximum_bitcast_fusion.1), calls=%async_computation | async-start | bytes 688128 | tf_op jit(solution)/shard_map/all_to_all | solution.py:83
  95.6 5.2 copy-start.33
  99.8 440.7 %copy-start.52 = (f32[1792]{0:T(1024)}, f32[1792]{0:T(1024)S(1)}, u32[]{:S(2)}) copy-start(f32[1792]{0:T(1024)S(1)} %get-tuple-element.250) | copy-start | bytes 21508
  99.8 621.4 %copy-start.55 = (f32[1792]{0:T(1024)}, f32[1792]{0:T(1024)S(1)}, u32[]{:S(2)}) copy-start(f32[1792]{0:T(1024)S(1)} %get-tuple-element.249) | copy-start | bytes 21508
  100.3 7.6 copy-start.76
  103.6 55.3 %all-to-all-start.2 = ((bf16[8,56,1216]{2,1,0:T(8,128)(2,1)}), bf16[8,56,1216]{2,1,0:T(8,128)(2,1)}, u32[]{:S(2)}, u32[]{:S(2)}) async-start(bf16[8,56,1216]{2,1,0:T(8,128)(2,1)} %maximum_bitcast_fusion), calls=%async_computation.2 | async-start | bytes 2293760 | tf_op jit(solution)/shard_map/all_to_all | solution.py:83
  107.9 138.9 %all-gather.21.cloned.1.call-start = ((), (), s32[]{:S(2)}) async-start(), calls=%async_computation.16 | async-start | bytes 5734400 | tf_op jit(solution)/shard_map/all_gather | solution.py:84
  109.2 58.7 %copy-start.11 = (f32[8,128,384]{2,1,0:T(8,128)}, f32[8,128,384]{2,1,0:T(8,128)S(1)}, u32[]{:S(2)}) copy-start(f32[8,128,384]{2,1,0:T(8,128)S(1)} %and_convert_fusion) | copy-start | bytes 4718596
  159.0 123.1 %all-gather.13.cloned.1.call-start = ((), (), s32[]{:S(2)}) async-start(), calls=%async_computation.12 | async-start | bytes 4128768 | tf_op jit(solution)/shard_map/all_gather | solution.py:51
  167.3 12.2 %copy-start.4 = (bf16[16,64,288]{2,1,0:T(8,128)(2,1)}, bf16[16,64,288]{2,1,0:T(8,128)(2,1)S(1)}, u32[]{:S(2)}) copy-start(bf16[16,64,288]{2,1,0:T(8,128)(2,1)S(1)} %broadcast_select_fusion.1) | copy-start | bytes 1769476
  234.7 96.4 %all-gather.15.cloned.1.call-start = ((), (), s32[]{:S(2)}) async-start(), calls=%async_computation.13 | async-start | bytes 2723840 | tf_op jit(solution)/shard_map/all_gather | solution.py:194
  236.4 129.7 %all-gather.23.cloned.1.call-start = ((), (), s32[]{:S(2)}) async-start(), calls=%async_computation.17 | async-start | bytes 4128768 | tf_op jit(solution)/shard_map/all_gather | solution.py:51
  374.4 9.7 copy-start.101
  374.4 9.7 copy-start.102
  384.1 48.2 %all-to-all-start.4 = ((bf16[8,128,1792]{2,1,0:T(8,128)(2,1)}), bf16[8,128,1792]{2,1,0:T(8,128)(2,1)}, u32[]{:S(2)}, u32[]{:S(2)}) async-start(bf16[8,128,1792]{2,1,0:T(8,128)(2,1)} %bitcast.366), calls=%async_computation.4 | async-start | bytes 7340032 | tf_op jit(solution)/shard_map/all_to_all | solution.py:56
  432.3 48.0 %all-to-all-start.3 = ((bf16[8,128,1792]{2,1,0:T(8,128)(2,1)}), bf16[8,128,1792]{2,1,0:T(8,128)(2,1)}, u32[]{:S(2)}, u32[]{:S(2)}) async-start(bf16[8,128,1792]{2,1,0:T(8,128)(2,1)} %bitcast.365), calls=%async_computation.3 | async-start | bytes 7340032 | tf_op jit(solution)/shard_map/all_to_all | solution.py:56
  480.3 51.8 %all-to-all-start.11 = ((bf16[4,152,1792]{2,1,0:T(8,128)(2,1)}), bf16[4,152,1792]{2,1,0:T(8,128)(2,1)}, u32[]{:S(2)}, u32[]{:S(2)}) async-start(bf16[4,152,1792]{2,1,0:T(8,128)(2,1)} %bitcast.368), calls=%async_computation.11 | async-start | bytes 4358144 | tf_op jit(solution)/shard_map/all_to_all | solution.py:100
  532.1 106.1 %all-to-all-start.9 = ((bf16[1,8,4,56,1216]{4,3,1,0,2:T(8,128)(2,1)}), bf16[1,8,4,56,1216]{4,3,1,0,2:T(8,128)(2,1)}, u32[]{:S(2)}, u32[]{:S(2)}) async-start(bf16[1,8,4,56,1216]{4,3,1,0,2:T(8,128)(2,1)} %copy.371), calls=%async_computation.9 | async-start | bytes 9175040 | tf_op jit(solution)/shard_map/all_to_all | solution.py:91
  537.1 133.2 %all-gather.17.cloned.1.call-start = ((), (), s32[]{:S(2)}) async-start(), calls=%async_computation.14 | async-start | bytes 4128768 | tf_op jit(solution)/shard_map/all_gather | solution.py:51
  540.4 10.0 %copy-start.89 = (f32[2,3,56]{2,0,1:T(2,128)S(1)}, f32[2,3,56]{2,0,1:T(2,128)}, u32[]{:S(2)}) copy-start(f32[2,3,56]{2,0,1:T(2,128)} %param.45) | copy-start | bytes 4036
  541.3 10.8 %copy-start.90 = (f32[128]{0:T(128)}, f32[128]{0:T(128)S(1)}, u32[]{:S(2)}) copy-start(f32[128]{0:T(128)S(1)} %broadcast_multiply_fusion.1) | copy-start | bytes 1540
  557.9 93.2 %copy-start.5 = (f32[152,1792]{1,0:T(8,128)}, f32[152,1792]{1,0:T(8,128)S(1)}, u32[]{:S(2)}) copy-start(f32[152,1792]{1,0:T(8,128)S(1)} %convert_reduce_fusion.4) | copy-start | bytes 3268612
  642.6 21.5 %all-to-all-start.10 = ((bf16[8,56,1216]{2,1,0:T(8,128)(2,1)}), bf16[8,56,1216]{2,1,0:T(8,128)(2,1)}, u32[]{:S(2)}, u32[]{:S(2)}) async-start(bf16[8,56,1216]{2,1,0:T(8,128)(2,1)} %reduce_sum.346), calls=%async_computation.10 | async-start | bytes 2293760 | tf_op jit(solution)/shard_map/all_to_all | solution.py:93
  665.7 8.9 copy-start.14
  670.3 7.3 copy-start.83
  707.5 10.1 %copy-start.65 = (f32[1,224]{1,0:T(1,128)S(1)}, f32[1,224]{1,0:T(1,128)}, u32[]{:S(2)}) copy-start(f32[1,224]{1,0:T(1,128)} %get-tuple-element.316) | copy-start | bytes 2692
  707.5 10.1 %copy-start.67 = (f32[1,224]{1,0:T(1,128)S(1)}, f32[1,224]{1,0:T(1,128)}, u32[]{:S(2)}) copy-start(f32[1,224]{1,0:T(1,128)} %get-tuple-element.317) | copy-start | bytes 2692
  729.5 34.5 %all-to-all-start.6 = ((bf16[1,8,4,56,288]{4,3,1,0,2:T(8,128)(2,1)}), bf16[1,8,4,56,288]{4,3,1,0,2:T(8,128)(2,1)}, u32[]{:S(2)}, u32[]{:S(2)}) async-start(bf16[1,8,4,56,288]{4,3,1,0,2:T(8,128)(2,1)} %copy.363), calls=%async_computation.6 | async-start | bytes 2752512 | tf_op jit(solution)/shard_map/all_to_all | solution.py:91
  743.1 6.9 copy-start.26
  743.1 6.9 copy-start.99
  764.0 26.0 %all-to-all-start.8 = ((bf16[4,56,1792]{2,1,0:T(8,128)(2,1)}), bf16[4,56,1792]{2,1,0:T(8,128)(2,1)}, u32[]{:S(2)}, u32[]{:S(2)}) async-start(bf16[4,56,1792]{2,1,0:T(8,128)(2,1)} %bitcast.375), calls=%async_computation.8 | async-start | bytes 1605632 | tf_op jit(solution)/shard_map/all_to_all | solution.py:100
  772.3 22.9 %copy-start.39 = (bf16[1792,288]{0,1:T(8,128)(2,1)S(1)}, bf16[1792,288]{0,1:T(8,128)(2,1)}, u32[]{:S(2)}) copy-start(bf16[1792,288]{0,1:T(8,128)(2,1)} %copy-done.38) | copy-start | bytes 3096580
  772.3 22.9 %copy-start.41 = (bf16[16,64,288]{2,1,0:T(8,128)(2,1)S(1)}, bf16[16,64,288]{2,1,0:T(8,128)(2,1)}, u32[]{:S(2)}) copy-start(bf16[16,64,288]{2,1,0:T(8,128)(2,1)} %copy-done.40) | copy-start | bytes 1769476
  790.0 12.9 %all-to-all-start.7 = ((bf16[8,56,288]{2,1,0:T(8,128)(2,1)}), bf16[8,56,288]{2,1,0:T(8,128)(2,1)S(1)}, u32[]{:S(2)}, u32[]{:S(2)}) async-start(bf16[8,56,288]{2,1,0:T(8,128)(2,1)} %reduce_sum.341), calls=%async_computation.7 | async-start | bytes 688128 | tf_op jit(solution)/shard_map/all_to_all | solution.py:93
  803.0 4.7 copy-start.61
  803.0 4.7 copy-start.62
  803.0 4.7 copy-start.63
  803.0 7.8 copy-start.28
  803.0 48.1 %all-to-all-start.5 = ((bf16[8,128,1792]{2,1,0:T(8,128)(2,1)}), bf16[8,128,1792]{2,1,0:T(8,128)(2,1)}, u32[]{:S(2)}, u32[]{:S(2)}) async-start(bf16[8,128,1792]{2,1,0:T(8,128)(2,1)} %bitcast.364), calls=%async_computation.5 | async-start | bytes 7340032 | tf_op jit(solution)/shard_map/all_to_all | solution.py:56
  818.1 35.6 %copy-start.56 = (f32[1792]{0:T(1024)S(1)}, f32[1792]{0:T(1024)}, u32[]{:S(2)}) copy-start(f32[1792]{0:T(1024)} %copy-done.55) | copy-start | bytes 21508
  818.1 35.6 %copy-start.92 = (f32[128]{0:T(128)S(1)}, f32[128]{0:T(128)}, u32[]{:S(2)}) copy-start(f32[128]{0:T(128)} %add_rsqrt_fusion.1) | copy-start | bytes 1540
  818.1 35.9 %copy-start.60 = (f32[1,1792]{1,0:T(1,128)S(1)}, f32[1,1792]{1,0:T(1,128)}, u32[]{:S(2)}) copy-start(f32[1,1792]{1,0:T(1,128)} %stack.133) | copy-start | bytes 21508
  818.1 78.2 %copy-start.87 = (f32[2,56]{1,0:T(2,128)S(1)}, f32[2,56]{1,0:T(2,128)}, u32[]{:S(2)}) copy-start(f32[2,56]{1,0:T(2,128)} %param.47) | copy-start | bytes 1348
  818.2 78.2 %copy-start.88 = (f32[2,56]{1,0:T(2,128)S(1)}, f32[2,56]{1,0:T(2,128)}, u32[]{:S(2)}) copy-start(f32[2,56]{1,0:T(2,128)} %param.43) | copy-start | bytes 1348
  818.2 83.9 %copy-start.97 = (f32[7]{0:T(128)S(1)}, f32[7]{0:T(128)}, u32[]{:S(2)}) copy-start(f32[7]{0:T(128)} %stack.155) | copy-start | bytes 88
  818.2 132.7 %copy-start.2 = (f32[128,1792]{1,0:T(8,128)S(1)}, f32[128,1792]{1,0:T(8,128)}, u32[]{:S(2)}) copy-start(f32[128,1792]{1,0:T(8,128)} %copy-done.1) | copy-start | bytes 2752516
  818.2 132.7 %copy-start.53 = (f32[1792]{0:T(1024)S(1)}, f32[1792]{0:T(1024)}, u32[]{:S(2)}) copy-start(f32[1792]{0:T(1024)} %copy-done.52) | copy-start | bytes 21508
  818.2 132.7 %copy-start.75 = (f32[128]{0:T(128)S(1)}, f32[128]{0:T(128)}, u32[]{:S(2)}) copy-start(f32[128]{0:T(128)} %copy-done.73) | copy-start | bytes 1540
  818.2 132.7 %copy-start.91 = (f32[128]{0:T(128)S(1)}, f32[128]{0:T(128)}, u32[]{:S(2)}) copy-start(f32[128]{0:T(128)} %copy-done.90) | copy-start | bytes 1540
  941.2 12.8 %copy-start.57 = (f32[2,7]{1,0:T(2,128)}, f32[2,7]{1,0:T(2,128)S(1)}, u32[]{:S(2)}) copy-start(f32[2,7]{1,0:T(2,128)S(1)} %sqrt.31) | copy-start | bytes 172
  950.9 4.3 copy-start.94
  950.9 4.8 copy-start.16
  950.9 4.8 copy-start.30
  950.9 5.6 copy-start.69
  950.9 5.6 copy-start.71
  950.9 6.2 copy-start.34
  950.9 6.2 copy-start.35
  951.0 7.5 copy-start.10
  954.0 4.4 copy-start.9
  (56 other events, 143.9 us)
Sparse Core Ops, SparseCore 0:
  9.9 37.5 all-gather.18
  159.1 87.6 all-gather.20
  249.2 32.8 all-gather.12
  284.1 46.9 all-gather.14
  332.8 33.1 all-gather.22
  542.6 36.9 all-gather.16
